TPU v7x, 32 devices: a whole 2x2x4 slice. The times are simulated.
32 devices in a mesh: gx: 8 (over y, x, core), gy: 4 (over z).
Axes of the slice: x: 2, y: 2, z: 4, core: 2. Of those that a mesh axis runs over, the one named last changes fastest.
Arguments:
- density: float32 [32, 256, 256], P(('gx', 'gy')), may hold values from -0.06 to 0.56, as said below
- coupling: float32 [32, 256, 256], P(('gx', 'gy')), may hold values from -0.04 to 0.04
- weights: float32 [32], P(('gx', 'gy')), may hold values from 0.25 to 2
- live_mask: int32 [32], P(('gx', 'gy')), may hold values 0 or 1
- dimer_pairs: int32 [32, 2], replicated, may hold values from 0 to 31, as said below
- dimer_slot: int32 [32], replicated, may hold values from 0 to 31, as said below
- frag_slot: int32 [32], replicated, may hold values from 0 to 31, as said below
Outputs:
- refined: float32 [32, 256, 256], P(('gx', 'gy'))
Inputs may be any that keep to these rules, and one draw needn't show every extreme that they name: `dimer_slot`: each slot holds exactly one listed dimer. `frag_slot`: each fragment has its own slot; slot q lies on device q, devices numbered with gy fastest. `dimer_pairs`: the two fragments of a dimer differ. The dimers in slots k * 1 to (k + 1) - 1 (device k) name 2 fragments whose storage devices have pairwise different gx indices and pairwise different gy indices. `density`: each block is symmetric.
All inputs are finite; a program needn't handle non-finite values. No bound on the sum of `live_mask` on one device may be relied on, other than what follows from the above.
Results may differ from a plain program's by a relative error of at most 0.0003.
Values sent between devices are 32-bit elements; how exact they have to be, the bound alone decides.
A program may use at most 64 MiB of HBM per device.

v0:
```python
import jax
import jax.numpy as jnp
from jax import lax
from jax.sharding import PartitionSpec as P

ITERS = 3


exact_precision = lax.Precision.HIGHEST


def product(left, right):
    return jnp.dot(left, right, precision=exact_precision, preferred_element_type=jnp.float32)


def purify(first_block, second_block, coupling_block):
    half_width = first_block.shape[0]
    upper_rows = jnp.concatenate([first_block, coupling_block], axis=1)
    lower_rows = jnp.concatenate([coupling_block.T, second_block], axis=1)
    matrix = jnp.concatenate([upper_rows, lower_rows], axis=0)
    for repeat in range(ITERS):
        square = product(matrix, matrix)
        matrix = 3.0 * square - 2.0 * product(square, matrix)
    return (matrix[:half_width, :half_width], matrix[half_width:, half_width:])


def running(operands):
    return purify(operands[0], operands[1], operands[2])


def resting(operands):
    return (jnp.zeros_like(operands[0]), jnp.zeros_like(operands[1]))


def dimer_increments(pieces, coupling, weights, live_mask):
    outputs = []
    factors = []
    for position in range(coupling.shape[0]):
        active = live_mask[position] > 0
        operands = (pieces[2 * position], pieces[2 * position + 1], coupling[position])
        first_new, second_new = lax.cond(active, running, resting, operands)
        factor = jnp.where(active, weights[position], jnp.float32(0.0))
        outputs = outputs + [factor * first_new, factor * second_new]
        factors = factors + [factor, factor]
    return (jnp.stack(outputs), jnp.stack(factors))


def routing(dimer_pairs, dimer_slot, frag_slot, frag_dev, count_x, count_y, refs):
    dimers = dimer_slot.shape[0]
    slot_ids = jnp.arange(dimers, dtype=jnp.int32)
    matches = dimer_slot[:, None] == slot_ids[None, :]
    slot_pairs = jnp.sum(jnp.where(matches[:, :, None], dimer_pairs[:, None, :], 0), axis=0)
    ref_slot = jnp.take(frag_slot, slot_pairs.reshape(-1), axis=0)
    owner = ref_slot // frag_dev
    layout = (count_x, count_y, refs)
    return (
        (owner // count_y).reshape(layout),
        (owner % count_y).reshape(layout),
        (ref_slot % frag_dev).reshape(layout),
    )


def selection(peer_match, peer_held, peer_local, own_index, frag_dev):
    found = peer_match == own_index
    valid = jnp.any(found, axis=1)
    pick = jnp.sum(jnp.where(found, peer_held * frag_dev + peer_local, 0), axis=1)
    return (valid, pick)


def send_pieces(held, valid, pick):
    return jnp.where(valid[:, None, None], jnp.take(held, pick, axis=0), jnp.float32(0.0))


def route_back(increments, factors, own_coord, peers):
    table = (own_coord[:, None] == jnp.arange(peers, dtype=jnp.int32)[None, :]).astype(jnp.float32)
    blocks = jnp.einsum("ra,rij->aij", table, increments, precision=exact_precision)
    sums = jnp.dot(factors, table, precision=exact_precision)
    return (blocks, sums)


def land(returned, returned_sums, valid, pick, held_count):
    hits = (pick[:, None] == jnp.arange(held_count, dtype=jnp.int32)[None, :]) & valid[:, None]
    table = hits.astype(jnp.float32)
    blocks = jnp.einsum("ah,aij->hij", table, returned, precision=exact_precision)
    sums = jnp.dot(returned_sums, table, precision=exact_precision)
    return (blocks, sums)


def per_device(density, coupling, weights, live_mask, dimer_pairs, dimer_slot, frag_slot):
    frag_dev = density.shape[0]
    refs = 2 * coupling.shape[0]
    count_x = lax.axis_size("gx")
    count_y = lax.axis_size("gy")
    index_x = lax.axis_index("gx")
    index_y = lax.axis_index("gy")
    owner_x, owner_y, owner_local = routing(
        dimer_pairs, dimer_slot, frag_slot, frag_dev, count_x, count_y, refs
    )
    mine_x = owner_x[index_x, index_y]
    blocks = density
    held = lax.all_gather(blocks, "gy", axis=0, tiled=True)
    valid, pick = selection(
        owner_x[:, index_y], owner_y[:, index_y], owner_local[:, index_y], index_x, frag_dev
    )
    incoming = lax.all_to_all(
        send_pieces(held, valid, pick), "gx", split_axis=0, concat_axis=0, tiled=True
    )
    increments, factors = dimer_increments(
        jnp.take(incoming, mine_x, axis=0), coupling, weights, live_mask
    )
    back_blocks, back_sums = route_back(increments, factors, mine_x, count_x)
    returned = lax.all_to_all(back_blocks, "gx", split_axis=0, concat_axis=0, tiled=True)
    returned_sums = lax.all_to_all(back_sums, "gx", split_axis=0, concat_axis=0, tiled=True)
    partial_blocks, partial_sums = land(returned, returned_sums, valid, pick, count_y * frag_dev)
    totals = lax.psum_scatter(partial_blocks, "gy", scatter_dimension=0, tiled=True)
    weight_sums = lax.psum_scatter(partial_sums, "gy", scatter_dimension=0, tiled=True)
    blocks = (blocks + totals) / (1.0 + weight_sums)[:, None, None]
    return blocks


def solution(mesh):
    return jax.shard_map(
        per_device,
        mesh=mesh,
        in_specs=(
            P(("gx", "gy"), None, None),
            P(("gx", "gy"), None, None),
            P(("gx", "gy")),
            P(("gx", "gy")),
            P(),
            P(),
            P(),
        ),
        out_specs=P(("gx", "gy"), None, None),
        check_vma=False,
    )
```

profile of v0, /device:TPU:0, one launch (start us, length us, event | category | flops | bytes accessed | tf_op | source)
XLA Modules:
  0.0 155.3 jit_solution(810021223028909148)
XLA Ops:
  6.5 0.7 all-gather.2.cloned.1.call-update
  7.3 0.7 iota_compare_fusion
  8.0 0.8 select_reduce_fusion
  9.1 0.8 gather_fusion.1
  10.3 0.2 fusion.14
  10.6 29.1 %all-gather.2.cloned.1.call-done = f32[4,256,256]{2,1,0:T(8,128)} async-done(((f32[1,256,256]{2,1,0:T(8,128)}), f32[4,256,256]{2,1,0:T(8,128)}) %all-gather.2.cloned.1.call-update) | async-done | bytes 1048592 | tf_op jit(solution)/shard_map/all_gather | solution.py:101
  39.7 1.9 %gather_fusion.2 = f32[8,256,256]{2,1,0:T(8,128)S(1)} fusion(f32[4,256,256]{2,1,0:T(8,128)} %all-gather.2.cloned.1.call-done, s32[1024]{0:T(1024)S(1)} %pad_clamp_fusion.1), kind=kCustom, calls=%fused_computation.2 | custom fusion | bytes 4194336 | tf_op jit(solution)/shard_map/jit(_take)/gather | solution.py:71
  41.6 1.7 %select_select_fusion = f32[8,256,256]{2,1,0:T(8,128)} fusion(f32[8,256,256]{2,1,0:T(8,128)S(1)} %gather_fusion.2, pred[8]{0:T(512)(128)(4,1)S(1)} %compare_and_fusion.1, pred[8]{0:T(512)(128)(4,1)S(1)} %get-tuple-element.125), kind=kLoop, calls=%fused_computation.23 | loop fusion | flops 1048576 | bytes 4194320 | tf_op jit(solution)/shard_map/jit(_where)/select_n | solution.py:71
  43.2 3.8 %all-to-all-start = ((f32[8,256,256]{2,1,0:T(8,128)}), f32[8,256,256]{2,1,0:T(8,128)S(1)}, u32[]{:S(2)}, u32[]{:S(2)}) async-start(f32[8,256,256]{2,1,0:T(8,128)} %select_select_fusion), calls=%async_computation | async-start | bytes 4194304 | tf_op jit(solution)/shard_map/all_to_all | solution.py:105
  48.6 25.1 %all-to-all-done = f32[8,256,256]{2,1,0:T(8,128)S(1)} async-done(((f32[8,256,256]{2,1,0:T(8,128)}), f32[8,256,256]{2,1,0:T(8,128)S(1)}, u32[]{:S(2)}, u32[]{:S(2)}) %all-to-all-start) | async-done | bytes 2097184 | tf_op jit(solution)/shard_map/all_to_all | solution.py:105
  73.6 12.5 %conditional.1 = (f32[256,256]{1,0:T(8,128)S(1)}, f32[256,256]{1,0:T(8,128)S(1)}) conditional(s32[]{:T(128)} %bitcast.10, () %tuple.20, (s32[2]{0:T(128)S(1)}, s32[1,1,2]{1,0,2:T(1,128)S(1)}, f32[8,256,256]{2,1,0:T(8,128)S(1)}, f32[1,256,256]{2,1,0:T(8,128)S(1)}) %tuple.39), branch_computations={%region_3.4_spmd, %region_4.5_spmd} | conditional | flops 9667740672 | bytes 20451404 | solution.py:41
  73.8 0.6 gather_fusion
  74.7 1.8 %fusion.3 = f32[512,512]{1,0:T(8,128)S(1)} fusion(f32[256,256]{1,0:T(8,128)S(1)} %get-tuple-element.135, f32[256,256]{1,0:T(8,128)S(1)} %copy.43, f32[256,256]{1,0:T(8,128)S(1)} %bitcast.53, f32[256,256]{1,0:T(8,128)S(1)} %get-tuple-element.134), kind=kOutput, calls=%fused_computation.10 | convolution fusion | flops 1611399168 | bytes 2097152 | tf_op jit(solution)/shard_map/cond/branch_1_fun/dot_general | solution.py:13
  76.5 1.9 %fusion.2 = f32[512,512]{1,0:T(8,128)S(1)} fusion(f32[512,512]{1,0:T(8,128)S(1)} %fusion.3, f32[256,256]{1,0:T(8,128)S(1)} %get-tuple-element.135, f32[256,256]{1,0:T(8,128)S(1)} %copy.43, f32[256,256]{1,0:T(8,128)S(1)} %bitcast.54, f32[256,256]{1,0:T(8,128)S(1)} %get-tuple-element.134), kind=kOutput, calls=%fused_computation.8 | convolution fusion | flops 1612185600 | bytes 3145728 | tf_op jit(solution)/shard_map/cond/branch_1_fun/dot_general | solution.py:13
  78.4 1.8 %fusion.38 = f32[512,512]{1,0:T(8,128)S(1)} fusion(f32[512,512]{1,0:T(8,128)S(1)} %fusion.2), kind=kOutput, calls=%fused_computation.78 | convolution fusion | flops 1610612736 | bytes 2097152 | tf_op jit(solution)/shard_map/cond/branch_1_fun/dot_general | solution.py:13
  80.3 1.9 %fusion.1 = f32[512,512]{1,0:T(8,128)S(1)} fusion(f32[512,512]{1,0:T(8,128)S(1)} %fusion.38, f32[512,512]{1,0:T(8,128)S(1)} %fusion.2), kind=kOutput, calls=%fused_computation.6 | convolution fusion | flops 1611399168 | bytes 3145728 | tf_op jit(solution)/shard_map/cond/branch_1_fun/dot_general | solution.py:13
  82.2 1.8 %fusion.39 = f32[512,512]{1,0:T(8,128)S(1)} fusion(f32[512,512]{1,0:T(8,128)S(1)} %fusion.1), kind=kOutput, calls=%fused_computation.79 | convolution fusion | flops 1610612736 | bytes 2097152 | tf_op jit(solution)/shard_map/cond/branch_1_fun/dot_general | solution.py:13
  84.0 1.9 %fusion = f32[512,512]{1,0:T(8,128)S(1)} fusion(f32[512,512]{1,0:T(8,128)S(1)} %fusion.39, f32[512,512]{1,0:T(8,128)S(1)} %fusion.1), kind=kOutput, calls=%fused_computation.4 | convolution fusion | flops 1611399168 | bytes 3145728 | tf_op jit(solution)/shard_map/cond/branch_1_fun/dot_general | solution.py:13
  86.1 0.3 copy.47
  86.6 1.7 %fusion.9 = f32[8,256,256]{2,0,1:T(8,128)S(1)} fusion(f32[1,256,256]{2,0,1:T(1,128)S(1)} %stack.15, f32[1,256,256]{2,0,1:T(1,128)S(1)} %copy.47, s32[2]{0:T(128)S(1)} %get-tuple-element.127), kind=kOutput, calls=%fused_computation.25 | convolution fusion | flops 12714000 | bytes 2621448 | tf_op jit(solution)/shard_map/ra,rij->aij/dot_general | solution.py:76
  88.4 0.7 copy.48
  89.1 29.0 %all_to_all.22 = f32[8,256,256]{2,1,0:T(8,128)S(1)} all-to-all(f32[8,256,256]{2,1,0:T(8,128)S(1)} %copy.48), channel_id=1, replica_groups=mesh['gx'=8,'gy'=4] {'gx'}, dimensions={0} | all-to-all | bytes 4194304 | tf_op jit(solution)/shard_map/all_to_all | solution.py:112
  118.1 2.2 %fusion.7 = f32[4,256,256]{2,0,1:T(4,128)S(1)} fusion(f32[8,256,256]{2,1,0:T(8,128)S(1)} %all_to_all.22, s32[8]{0:T(128)S(1)} %fusion.14, pred[8]{0:T(512)(128)(4,1)S(1)} %get-tuple-element.125), kind=kOutput, calls=%fused_computation.21 | convolution fusion | flops 25165888 | bytes 3145768 | tf_op jit(solution)/shard_map/ah,aij->hij/dot_general | solution.py:84
  120.3 1.2 copy.50
  121.5 0.9 fusion.21
  122.4 3.3 %all-to-all-start.2 = ((f32[8,1,1]{2,1,0:T(1,128)}), f32[8,1,1]{2,1,0:T(1,128)S(1)}, u32[]{:S(2)}, u32[]{:S(2)}) async-start(f32[8,1,1]{2,1,0:T(1,128)} %bitcast.23), calls=%async_computation.3 | async-start | bytes 8192 | tf_op jit(solution)/shard_map/all_to_all | solution.py:113
  125.7 4.5 %all-to-all-done.2 = f32[8,1,1]{2,1,0:T(1,128)S(1)} async-done(((f32[8,1,1]{2,1,0:T(1,128)}), f32[8,1,1]{2,1,0:T(1,128)S(1)}, u32[]{:S(2)}, u32[]{:S(2)}) %all-to-all-start.2) | async-done | bytes 64 | tf_op jit(solution)/shard_map/all_to_all | solution.py:113
  130.5 0.6 dynamic-slice
  131.1 10.5 %all-reduce = f32[4]{0:T(128)S(1)} all-reduce(f32[4]{0:T(128)S(1)} %convolution_bitcast_fusion), channel_id=3, replica_groups=mesh['gx'=8,'gy'=4] {'gy'}, use_global_device_ids=true, to_apply=%region_6.7.clone | all-reduce | flops 4 | bytes 32
  141.6 1.2 dynamic-slice.1
  143.5 3.3 %reduce-scatter.2.cloned.1.call-done = f32[1,256,256]{2,1,0:T(8,128)} async-done(((f32[4,256,256]{2,1,0:T(8,128)}), f32[1,256,256]{2,1,0:T(8,128)}) %reduce-scatter.2.cloned.1.call-update) | async-done | bytes 262160 | tf_op jit(solution)/shard_map/reduce_scatter | solution.py:115
  146.8 1.7 %add_divide_fusion = f32[1,256,256]{2,1,0:T(8,128)} fusion(f32[1,256,256]{2,1,0:T(8,128)S(1)} %copy-done.1, f32[1,256,256]{2,1,0:T(8,128)} %reduce-scatter.2.cloned.1.call-done, f32[]{:T(128)} %bitcast.18), kind=kLoop, calls=%fused_computation.29 | loop fusion | flops 131072 | bytes 786436 | tf_op jit(solution)/shard_map/div | solution.py:117
  (37 shorter events, 2.0 us)
Async XLA Ops:
  6.5 2.5 %copy-start = (s32[32]{0:T(128)S(1)}, s32[32]{0:T(128)}, u32[]{:S(2)}) copy-start(s32[32]{0:T(128)} %param.15) | copy-start | bytes 388
  6.5 33.1 %all-gather.2.cloned.1.call-start = ((), (), s32[]{:S(2)}) async-start(), calls=%async_computation.4 | async-start | bytes 1310720 | tf_op jit(solution)/shard_map/all_gather | solution.py:101
  43.2 30.4 %copy-start.2 = (f32[1,256,256]{2,1,0:T(8,128)S(1)}, f32[1,256,256]{2,1,0:T(8,128)}, u32[]{:S(2)}) copy-start(f32[1,256,256]{2,1,0:T(8,128)} %param.10) | copy-start | bytes 786436
  43.2 30.4 %all-to-all-start = ((f32[8,256,256]{2,1,0:T(8,128)}), f32[8,256,256]{2,1,0:T(8,128)S(1)}, u32[]{:S(2)}, u32[]{:S(2)}) async-start(f32[8,256,256]{2,1,0:T(8,128)} %select_select_fusion), calls=%async_computation | async-start | bytes 4194304 | tf_op jit(solution)/shard_map/all_to_all | solution.py:105
  47.0 99.8 %reduce-scatter.2.cloned.1.call-start = ((), (), s32[]{:S(2)}) async-start(), calls=%async_computation.5 | async-start | bytes 1310720 | tf_op jit(solution)/shard_map/reduce_scatter | solution.py:115
  120.3 10.2 %copy-start.3 = (u32[32]{0:T(128)S(1)}, u32[32]{0:T(128)}, u32[]{:S(2)}) copy-start(u32[32]{0:T(128)} %constant.131) | copy-start | bytes 388
  120.3 26.5 %copy-start.1 = (f32[1,256,256]{2,1,0:T(8,128)S(1)}, f32[1,256,256]{2,1,0:T(8,128)}, u32[]{:S(2)}) copy-start(f32[1,256,256]{2,1,0:T(8,128)} %param.9) | copy-start | bytes 786436
  122.4 7.9 %all-to-all-start.2 = ((f32[8,1,1]{2,1,0:T(1,128)}), f32[8,1,1]{2,1,0:T(1,128)S(1)}, u32[]{:S(2)}, u32[]{:S(2)}) async-start(f32[8,1,1]{2,1,0:T(1,128)} %bitcast.23), calls=%async_computation.3 | async-start | bytes 8192 | tf_op jit(solution)/shard_map/all_to_all | solution.py:113
Sparse Core Ops, SparseCore 0:
  8.9 30.7 all-gather.1
  121.6 25.0 reduce-scatter.1
where the time goes:
time: 156 us; the launch traced here: 155 us
  waiting for transfers between devices  62.8 us (40%)
  blocking collectives  39.5 us (25%)
  matrix products  16.1 us (10%)
  between operations  15.5 us (10%)
  local copies, waits for them, and re-layouts  8.44 us (5%)
  starting transfers between devices  7.14 us (5%)
  other arithmetic  5.63 us (4%)
    all_gather x1, waiting for transfers between devices, per_device(): held = lax.all_gather(blocks, 'gy', axis=0, tiled=True)  29.1 us
    all_to_all x1, blocking collectives, per_device(): lax.all_to_all(back_blocks, 'gx', split_axis=0, concat_axis=0, tiled=True)  29 us
    all_to_all x1, waiting for transfers between devices, per_device(): lax.all_to_all(send_pieces(held, valid, pick), 'gx', split_axis=0, concat...  25.1 us
    dot_general x6, matrix products, product(): jnp.dot(left, right, precision=exact_precision, preferred_element_type=jn...  11.2 us
    unnamed x1, blocking collectives  10.5 us
    all_to_all x1, waiting for transfers between devices, per_device(): lax.all_to_all(back_sums, 'gx', split_axis=0, concat_axis=0, tiled=True)  4.54 us
    all_to_all x1, starting transfers between devices, per_device(): lax.all_to_all(send_pieces(held, valid, pick), 'gx', split_axis=0, concat...  3.79 us
    reduce_scatter x1, waiting for transfers between devices, per_device(): lax.psum_scatter(partial_blocks, 'gy', scatter_dimension=0, tiled=True)  3.33 us
  transfers between devices with their start and end apart: 4, of which 4 were waited for; matrix products, arithmetic and copies ran while one was open for 4% of the time, Pallas kernels for 0%

commit v1 on v0

v1 whole, which is shorter than its diff:
```python
import functools
import jax
import jax.numpy as jnp
from jax import lax
from jax.experimental import pallas as pl
from jax.experimental.pallas import tpu as pltpu
from jax.sharding import PartitionSpec as P

ITERS = 3
MESH = pl.DeviceIdType.MESH
F32 = jnp.float32
BF16 = jnp.bfloat16


def split(value):
    high = value.astype(BF16)
    return high, (value - high.astype(F32)).astype(BF16)


def mm(left, right):
    return jnp.dot(left, right, preferred_element_type=F32)


def wrap(index, count):
    return jnp.where(index < 0, index + count, index)


def grid_iota(rows, columns):
    return (
        lax.broadcasted_iota(jnp.int32, (rows, columns), 0),
        lax.broadcasted_iota(jnp.int32, (rows, columns), 1),
    )


def kernel(
    count_x, count_y,
    density_ref, coupling_ref, weights_ref, live_ref, pairs_ref, dslot_ref, fslot_ref,
    out_ref,
    codes, refs_s, packed, held, diag, held_diag, chosen, got, joined,
    matrix, m_high, m_low, q_high, q_low, square,
    grown, landed, extra, landed_extra, flat, table, totals, back,
    send_sems, recv_sems,
):
    count = count_x * count_y
    dim_dev = coupling_ref.shape[0]
    refs = 2 * dim_dev
    dimers = dslot_ref.shape[0]
    width = density_ref.shape[1]
    half = width // 2
    rows = width // count
    me = lax.axis_index("gx") * count_y + lax.axis_index("gy")

    def peer(step):
        other = lax.rem(me + step, count)
        return other, (lax.div(other, count_y), lax.rem(other, count_y))

    barrier = pltpu.get_barrier_semaphore()

    def greet(step, carry):
        pl.semaphore_signal(barrier, inc=1, device_id=peer(step)[1], device_id_type=MESH)
        return carry

    lax.fori_loop(1, count, greet, 0)

    row_id, column_id = grid_iota(half, half)
    upper = row_id <= column_id
    strict = row_id > column_id
    on_diag = row_id == column_id

    def pack(first, corner, second):
        mixed = jnp.where(upper, first, second)
        return corner, mixed, jnp.sum(jnp.where(on_diag, second, 0.0), axis=0, keepdims=True)

    def scatter_rows(target, corner, mixed):
        for piece in range(count):
            start = piece * rows
            source = corner if start < half else mixed
            start = start % half
            target(piece, source[start:start + rows])

    corner, mixed, diag_row = pack(
        density_ref[0, :half, :half], density_ref[0, :half, half:], density_ref[0, half:, half:]
    )

    def put_packed(piece, value):
        packed[piece] = value

    scatter_rows(put_packed, corner, mixed)
    diag[...] = diag_row

    pl.semaphore_wait(barrier, count - 1)

    def exchange(phase, source, target, same):
        def send(step, carry):
            other, where_to = peer(step)
            pltpu.make_async_remote_copy(
                src_ref=source if same else source.at[other],
                dst_ref=target.at[count - step],
                send_sem=send_sems.at[phase],
                recv_sem=recv_sems.at[phase],
                device_id=where_to,
                device_id_type=MESH,
            ).start()
            return carry

        lax.fori_loop(1, count, send, 0)

    def wait_for(sems, phase, target):
        span = target.at[pl.ds(1, count - 1)]
        pltpu.make_async_copy(span, span, sems.at[phase]).wait()

    exchange(0, packed, held, False)
    exchange(1, diag, held_diag, True)
    held[0] = packed[me]
    held_diag[0] = diag[...]

    def code_of(dimer, carry):
        codes[dimer] = fslot_ref[pairs_ref[dimer, 0]] * count + fslot_ref[pairs_ref[dimer, 1]]
        return carry

    lax.fori_loop(0, dimers, code_of, 0)

    def names(slot, carry):
        def look(dimer, found):
            return jnp.where(dslot_ref[dimer] == slot, codes[dimer], found)

        found = lax.fori_loop(0, dimers, look, jnp.int32(0), unroll=dimers <= 64)
        refs_s[2 * slot] = lax.div(found, jnp.int32(count))
        refs_s[2 * slot + 1] = lax.rem(found, jnp.int32(count))
        return carry

    lax.fori_loop(0, count * dim_dev, names, 0)

    wait_for(recv_sems, 0, held)

    def choose(target, carry):
        for ref in range(refs):
            slot = refs_s[target * refs + ref]
            chosen[target, ref] = held[wrap(slot - me, count)]
        return carry

    lax.fori_loop(0, count, choose, 0, unroll=count <= 32)
    exchange(2, chosen, got, False)
    got[0] = chosen[me]
    wait_for(recv_sems, 1, held_diag)

    lanes = count * refs * rows
    lane_id = lax.broadcasted_iota(jnp.int32, (1, lanes), 1)
    lane_ref = lane_id // rows

    def spread(entry, row):
        ref = lax.rem(entry, refs)
        source = lax.rem(me + lax.div(entry, refs), count)
        return jnp.where(lane_ref == entry, refs_s[source * refs + ref], row)

    named = lax.fori_loop(
        0, count * refs, spread, jnp.zeros((1, lanes), jnp.int32), unroll=count * refs <= 64
    )
    named = named * rows + lane_id % rows
    table_row = lax.broadcasted_iota(jnp.int32, (count * rows, lanes), 0)
    table[...] = jnp.where(table_row == named, 1.0, 0.0).astype(BF16)

    wait_for(recv_sems, 2, got)

    for dimer in range(dim_dev):
        coupled = coupling_ref[dimer]
        matrix[:width, width:] = coupled
        matrix[width:, :width] = coupled.T
        for side in range(2):
            ref = 2 * dimer + side
            for piece in range(count):
                joined[piece * rows:(piece + 1) * rows, :] = got[wrap(piece - me, count), ref]
            corner = joined[:half, :]
            mixed = joined[half:, :]
            turned = mixed.T
            slot = refs_s[me * refs + ref]
            diag_row = held_diag[wrap(slot - me, count)]
            low = side * width
            mid = low + half
            high = low + width
            matrix[low:mid, low:mid] = jnp.where(upper, mixed, turned)
            matrix[low:mid, mid:high] = corner
            matrix[mid:high, low:mid] = corner.T
            matrix[mid:high, mid:high] = jnp.where(
                on_diag, diag_row, jnp.where(strict, mixed, turned)
            )
        for repeat in range(ITERS):
            m_high[...], m_low[...] = split(matrix[...])
            square[...] = (
                mm(m_high[...], m_high[...])
                + mm(m_high[...], m_low[...])
                + mm(m_low[...], m_high[...])
            )
            q_high[...], q_low[...] = split(square[...])
            if repeat < ITERS - 1:
                cuts = ((slice(None), slice(None)),)
            else:
                cuts = tuple(
                    (slice(side * width, (side + 1) * width),) * 2 for side in range(2)
                )
            for across, down in cuts:
                cube = (
                    mm(q_high[across, :], m_high[:, down])
                    + mm(q_high[across, :], m_low[:, down])
                    + mm(q_low[across, :], m_high[:, down])
                )
                matrix[across, down] = 3.0 * square[across, down] - 2.0 * cube
        factor = jnp.where(live_ref[dimer] > 0, weights_ref[dimer], jnp.float32(0.0))
        for side in range(2):
            ref = 2 * dimer + side
            low = side * width
            mid = low + half
            high = low + width
            corner, mixed, diag_row = pack(
                factor * matrix[low:mid, low:mid],
                factor * matrix[low:mid, mid:high],
                factor * matrix[mid:high, mid:high],
            )

            def put_grown(piece, value, ref=ref):
                grown[piece, ref] = value

            scatter_rows(put_grown, corner, mixed)
            extra[ref:ref + 1, :] = diag_row
            extra[refs + ref:refs + ref + 1, :] = jnp.full((1, half), factor, F32)

    exchange(3, grown, landed, False)
    exchange(4, extra, landed_extra, True)
    landed[0] = grown[me]
    landed_extra[0] = extra[...]

    wait_for(recv_sems, 3, landed)
    if rows == 8:
        values = landed[...].reshape(lanes, half)
    else:
        for entry in range(count * refs):
            flat[entry * rows:(entry + 1) * rows, :] = landed[entry // refs, entry % refs]
        values = flat[...]
    first, rest = values.astype(BF16), None
    rest = values - first.astype(F32)
    second, third = split(rest)
    sums = mm(table[...], first) + mm(table[...], second) + mm(table[...], third)
    for piece in range(count):
        totals[piece] = sums[piece * rows:(piece + 1) * rows, :]
    exchange(5, totals, back, False)
    back[0] = totals[me]

    wait_for(recv_sems, 4, landed_extra)
    which = lax.broadcasted_iota(jnp.int32, (2 * refs, half), 0) % refs

    def collect(entry, carry):
        source = lax.rem(me + entry, count)
        mask = jnp.zeros((2 * refs, half), jnp.int32)
        for ref in range(refs):
            hit = jnp.where(refs_s[source * refs + ref] == me, 1, 0)
            mask = jnp.where(which == ref, hit, mask)
        return carry + jnp.where(mask > 0, landed_extra[entry], 0.0)

    side_sums = lax.fori_loop(
        0, count, collect, jnp.zeros((2 * refs, half), F32), unroll=count <= 32
    )
    diag_total = jnp.sum(side_sums[:refs], axis=0, keepdims=True)
    scale = 1.0 + jnp.sum(side_sums[refs:], axis=0, keepdims=True)

    wait_for(recv_sems, 5, back)
    for piece in range(count):
        joined[piece * rows:(piece + 1) * rows, :] = back[wrap(piece - me, count)]
    corner = joined[:half, :]
    mixed = joined[half:, :]
    turned = mixed.T
    out_ref[0, :half, :half] = (
        density_ref[0, :half, :half] + jnp.where(upper, mixed, turned)
    ) / scale
    out_ref[0, :half, half:] = (density_ref[0, :half, half:] + corner) / scale
    out_ref[0, half:, :half] = (density_ref[0, half:, :half] + corner.T) / scale
    out_ref[0, half:, half:] = (
        density_ref[0, half:, half:]
        + jnp.where(on_diag, diag_total, jnp.where(strict, mixed, turned))
    ) / scale

    for phase, target in enumerate((held, held_diag, got, landed, landed_extra, back)):
        wait_for(send_sems, phase, target)


def solution(mesh):
    count_x, count_y = mesh.shape["gx"], mesh.shape["gy"]
    count = count_x * count_y

    def per_device(density, coupling, weights, live_mask, dimer_pairs, dimer_slot, frag_slot):
        frag_dev, width, _ = density.shape
        dim_dev = coupling.shape[0]
        refs = 2 * dim_dev
        half = width // 2
        rows = width // count
        assert frag_dev == 1 and rows * count == width
        vmem = lambda *shape: pltpu.VMEM(shape, F32)
        bf16 = lambda *shape: pltpu.VMEM(shape, BF16)
        in_vmem = pl.BlockSpec(memory_space=pltpu.VMEM)
        in_smem = pl.BlockSpec(memory_space=pltpu.SMEM)
        return pl.pallas_call(
            functools.partial(kernel, count_x, count_y),
            out_shape=jax.ShapeDtypeStruct(density.shape, F32),
            in_specs=[in_vmem, in_vmem] + [in_smem] * 5,
            out_specs=in_vmem,
            scratch_shapes=[
                pltpu.SMEM((dimer_slot.shape[0],), jnp.int32),
                pltpu.SMEM((count * refs,), jnp.int32),
                vmem(count, rows, half),
                vmem(count, rows, half),
                vmem(1, half),
                vmem(count, 1, half),
                vmem(count, refs, rows, half),
                vmem(count, refs, rows, half),
                vmem(width, half),
                vmem(2 * width, 2 * width),
                bf16(2 * width, 2 * width),
                bf16(2 * width, 2 * width),
                bf16(2 * width, 2 * width),
                bf16(2 * width, 2 * width),
                vmem(2 * width, 2 * width),
                vmem(count, refs, rows, half),
                vmem(count, refs, rows, half),
                vmem(2 * refs, half),
                vmem(count, 2 * refs, half),
                vmem(count * refs * rows if rows != 8 else 8, half),
                bf16(count * rows, count * refs * rows),
                vmem(count, rows, half),
                vmem(count, rows, half),
                pltpu.SemaphoreType.DMA((6,)),
                pltpu.SemaphoreType.DMA((6,)),
            ],
            compiler_params=pltpu.CompilerParams(collective_id=0, has_side_effects=True),
        )(density, coupling, weights, live_mask, dimer_pairs, dimer_slot, frag_slot)

    both = ("gx", "gy")
    return jax.shard_map(
        per_device,
        mesh=mesh,
        in_specs=(
            P(both, None, None),
            P(both, None, None),
            P(both),
            P(both),
            P(),
            P(),
            P(),
        ),
        out_specs=P(both, None, None),
        check_vma=False,
    )
```

time: 156 us -> 46.5 us (0.30)
  waiting for transfers between devices: 62.8 us -> 0 us
  Pallas kernels: 0 us -> 42.6 us
  blocking collectives: 39.5 us -> 0 us
  matrix products: 16.1 us -> 0 us
  between operations: 15.5 us -> 1.33 us
  starting transfers between devices: 7.14 us -> 0 us
  local copies, waits for them, and re-layouts: 8.44 us -> 2.37 us
  other arithmetic: 5.63 us -> 0 us
    pallas_call x0 -> x1, Pallas kernels: none -> 42.6 us  [per_device(): pl.pallas_call(functools.partial(kernel, count_x, count_y), out_shape=jax...]
    all_to_all x2 -> x0, waiting for transfers between devices: 29.6 us -> none  [the longest x1 25.1 us: per_device(): lax.all_to_all(send_pieces(held, valid, pick), 'gx', split_axis=0, concat...]
    all_gather x1 -> x0, waiting for transfers between devices: 29.1 us -> none  [per_device(): held = lax.all_gather(blocks, 'gy', axis=0, tiled=True)]
    all_to_all x1 -> x0, blocking collectives: 29 us -> none  [per_device(): lax.all_to_all(back_blocks, 'gx', split_axis=0, concat_axis=0, tiled=True)]
    dot_general x10 -> x0, matrix products: 16.1 us -> none  [the longest x6 11.2 us: product(): jnp.dot(left, right, precision=exact_precision, preferred_element_type=jn...]
    unnamed x1 -> x0, blocking collectives: 10.5 us -> none
    all_to_all x2 -> x0, starting transfers between devices: 7.1 us -> none  [the longest x1 3.79 us: per_device(): lax.all_to_all(send_pieces(held, valid, pick), 'gx', split_axis=0, concat...]
    gather x5 -> x0, local copies, waits for them, and re-layouts: 3.51 us -> none  [the longest x1 1.9 us: send_pieces(): jnp.take(held, pick, axis=0)]
  transfers between devices with their start and end apart: 4 -> 0, of which waited for: 4 -> 0; matrix products, arithmetic and copies ran while one was open for 4% -> 0% of each run, Pallas kernels for 0% -> 0%
where the time goes in v1:
time: 46.5 us; the launch traced here: 46.3 us
  Pallas kernels  42.6 us (92%)
  local copies, waits for them, and re-layouts  2.37 us (5%)
  between operations  1.33 us (3%)
    pallas_call x1, Pallas kernels, per_device(): pl.pallas_call(functools.partial(kernel, count_x, count_y), out_shape=jax...  42.6 us
    unnamed x4, local copies, waits for them, and re-layouts  2.37 us

profile of v1, /device:TPU:0, one launch (start us, length us, event | category | flops | bytes accessed | tf_op | source)
XLA Modules:
  0.0 46.3 jit_solution(13291905577616631068)
XLA Ops:
  0.7 0.0 copy-start
  1.3 0.0 copy-done
  1.3 0.7 %copy.8.pairs_ref = s32[32,2]{1,0:T(8,128)} copy(s32[32,2]{0,1:T(2,128)S(1)} %copy-done) | data formatting | bytes 512 | tf_op args[4]
  2.0 42.6 %shard_map.73 = f32[1,256,256]{2,1,0:T(8,128)} custom-call(f32[1,256,256]{2,1,0:T(8,128)} %density_ref.1, f32[1,256,256]{2,1,0:T(8,128)} %coupling_ref.1, f32[1]{0:T(128)S(6)} %copy.10.weights_ref, s32[1]{0:T(128)S(6)} %copy.11.live_ref, s32[32,2]{1,0:T(8,128)} %copy.8.pairs_ref, s32[32]{0:T(128)} %dslot_ref.1, s32[32]{0:T(128)} %fslot_ref.1), custom_call_target="tpu_custom_call" | custom-call | tf_op jit(solution)/shard_map/pallas_call | solution.py:300
  44.6 1.7 %copy.12 = f32[1,256,256]{2,1,0:T(8,128)} copy(f32[1,256,256]{2,1,0:T(8,128)} %shard_map.73) | data formatting | bytes 524288
Async XLA Ops:
  0.7 0.7 %copy-start = (s32[32,2]{0,1:T(2,128)S(1)}, s32[32,2]{0,1:T(2,128)}, u32[]{:S(2)}) copy-start(s32[32,2]{0,1:T(2,128)} %param.11) | copy-start | bytes 772

commit v2 on v1

--- a/solution.py
+++ b/solution.py
@@ -34,12 +34,13 @@
 
 def kernel(
     count_x, count_y,
+    density_in, coupling_in, weights_in, live_in, pairs_in, dslot_in, fslot_in,
+    out_ref,
     density_ref, coupling_ref, weights_ref, live_ref, pairs_ref, dslot_ref, fslot_ref,
-    out_ref,
     codes, refs_s, packed, held, diag, held_diag, chosen, got, joined,
     matrix, m_high, m_low, q_high, q_low, square,
     grown, landed, extra, landed_extra, flat, table, totals, back,
-    send_sems, recv_sems,
+    send_sems, recv_sems, stage_sems,
 ):
     count = count_x * count_y
     dim_dev = coupling_ref.shape[0]
@@ -62,6 +63,18 @@
 
     lax.fori_loop(1, count, greet, 0)
 
+    staged = [
+        pltpu.make_async_copy(source, target, stage_sems.at[place])
+        for place, (source, target) in enumerate((
+            (density_in, density_ref), (dslot_in, dslot_ref), (fslot_in, fslot_ref),
+            (pairs_in, pairs_ref), (weights_in, weights_ref), (live_in, live_ref),
+            (coupling_in, coupling_ref),
+        ))
+    ]
+    for copy in staged:
+        copy.start()
+    staged[0].wait()
+
     row_id, column_id = grid_iota(half, half)
     upper = row_id <= column_id
     strict = row_id > column_id
@@ -91,7 +104,8 @@
     pl.semaphore_wait(barrier, count - 1)
 
     def exchange(phase, source, target, same):
-        def send(step, carry):
+        def send(turn, carry, lag):
+            step = turn * count_y + lag
             other, where_to = peer(step)
             pltpu.make_async_remote_copy(
                 src_ref=source if same else source.at[other],
@@ -103,7 +117,10 @@
             ).start()
             return carry
 
-        lax.fori_loop(1, count, send, 0)
+        for lag in sorted(range(count_y), key=lambda lag: -min(lag, count_y - lag)):
+            lax.fori_loop(
+                0 if lag else 1, count_x, functools.partial(send, lag=lag), 0, unroll=count_x <= 8
+            )
 
     def wait_for(sems, phase, target):
         span = target.at[pl.ds(1, count - 1)]
@@ -114,8 +131,11 @@
     held[0] = packed[me]
     held_diag[0] = diag[...]
 
+    for copy in staged[1:]:
+        copy.wait()
+
     def code_of(dimer, carry):
-        codes[dimer] = fslot_ref[pairs_ref[dimer, 0]] * count + fslot_ref[pairs_ref[dimer, 1]]
+        codes[dimer] = fslot_ref[pairs_ref[0, dimer]] * count + fslot_ref[pairs_ref[1, dimer]]
         return carry
 
     lax.fori_loop(0, dimers, code_of, 0)
@@ -160,12 +180,17 @@
     table_row = lax.broadcasted_iota(jnp.int32, (count * rows, lanes), 0)
     table[...] = jnp.where(table_row == named, 1.0, 0.0).astype(BF16)
 
-    wait_for(recv_sems, 2, got)
-
-    for dimer in range(dim_dev):
+    def couple(dimer):
         coupled = coupling_ref[dimer]
         matrix[:width, width:] = coupled
         matrix[width:, :width] = coupled.T
+
+    couple(0)
+    wait_for(recv_sems, 2, got)
+
+    for dimer in range(dim_dev):
+        if dimer:
+            couple(dimer)
         for side in range(2):
             ref = 2 * dimer + side
             for piece in range(count):
@@ -296,13 +321,21 @@
         vmem = lambda *shape: pltpu.VMEM(shape, F32)
         bf16 = lambda *shape: pltpu.VMEM(shape, BF16)
         in_vmem = pl.BlockSpec(memory_space=pltpu.VMEM)
-        in_smem = pl.BlockSpec(memory_space=pltpu.SMEM)
+        smem = lambda array: pltpu.SMEM(array.shape, array.dtype)
+        pairs = dimer_pairs.T
         return pl.pallas_call(
             functools.partial(kernel, count_x, count_y),
-            out_shape=jax.ShapeDtypeStruct(density.shape, F32),
-            in_specs=[in_vmem, in_vmem] + [in_smem] * 5,
+            out_shape=pltpu.VMEM(density.shape, F32),
+            in_specs=[pl.BlockSpec(memory_space=pl.ANY)] * 7,
             out_specs=in_vmem,
             scratch_shapes=[
+                vmem(*density.shape),
+                vmem(*coupling.shape),
+                smem(weights),
+                smem(live_mask),
+                smem(pairs),
+                smem(dimer_slot),
+                smem(frag_slot),
                 pltpu.SMEM((dimer_slot.shape[0],), jnp.int32),
                 pltpu.SMEM((count * refs,), jnp.int32),
                 vmem(count, rows, half),
@@ -328,9 +361,10 @@
                 vmem(count, rows, half),
                 pltpu.SemaphoreType.DMA((6,)),
                 pltpu.SemaphoreType.DMA((6,)),
+                pltpu.SemaphoreType.DMA((7,)),
             ],
             compiler_params=pltpu.CompilerParams(collective_id=0, has_side_effects=True),
-        )(density, coupling, weights, live_mask, dimer_pairs, dimer_slot, frag_slot)
+        )(density, coupling, weights, live_mask, pairs, dimer_slot, frag_slot)
 
     both = ("gx", "gy")
     return jax.shard_map(

time: 46.5 us -> 41.3 us (0.89)
  Pallas kernels: 42.6 us -> 39.1 us
  local copies, waits for them, and re-layouts: 2.37 us -> 0.71 us
    pallas_call x1, Pallas kernels: 42.6 us -> 39.1 us  [per_device(): pl.pallas_call(functools.partial(kernel, count_x, count_y), out_shape=plt...]
    unnamed x4 -> x1, local copies, waits for them, and re-layouts: 2.37 us -> 0.71 us
where the time goes in v2:
time: 41.3 us; the launch traced here: 41.1 us
  Pallas kernels  39.1 us (95%)
  between operations  1.3 us (3%)
  local copies, waits for them, and re-layouts  0.71 us (2%)
    pallas_call x1, Pallas kernels, per_device(): pl.pallas_call(functools.partial(kernel, count_x, count_y), out_shape=plt...  39.1 us

profile of v2, /device:TPU:0, one launch (start us, length us, event | category | flops | bytes accessed | tf_op | source)
XLA Modules:
  0.0 41.1 jit_solution(3541559275811659712)
XLA Ops:
  1.3 39.1 %shard_map.73 = f32[1,256,256]{2,1,0:T(8,128)S(1)} custom-call(f32[1,256,256]{2,1,0:T(8,128)} %density_in.1, f32[1,256,256]{2,1,0:T(8,128)} %coupling_in.1, f32[1]{0:T(128)S(6)} %copy.10.weights_in, s32[1]{0:T(128)S(6)} %copy.11.live_in, s32[2,32]{1,0:T(2,128)} %bitcast.1, s32[32]{0:T(128)} %dslot_in.1, s32[32]{0:T(128)} %fslot_in.1), custom_call_target="tpu_custom_call" | custom-call | tf_op jit(solution)/shard_map/pallas_call | solution.py:326
  40.4 0.7 %copy.9 = f32[1,256,256]{2,1,0:T(8,128)} copy(f32[1,256,256]{2,1,0:T(8,128)S(1)} %shard_map.73) | data formatting | bytes 524288
